TPU v7x, 32 devices: a whole 2x2x4 slice. The times are simulated.
32 devices in a mesh: row: 8 (over z, x), col: 4 (over y, core).
Axes of the slice: x: 2, y: 2, z: 4, core: 2. Of those that a mesh axis runs over, the one named last changes fastest.
Arguments:
- factor: float32 [9, 1024, 3, 512], P(None, 'row', None, 'col'), may hold values from -2 to 2.5, as said below
- adjoint: float32 [9, 1024, 3, 512], P(None, 'row', None, 'col'), may hold values from -6 to 6
Outputs:
- kernel_adjoint: float32 [9, 1024, 3, 512], P(None, 'row', None, 'col')
Inputs may be any that keep to these rules, and one draw needn't show every extreme that they name: `factor`: zero where the column minus 512 exceeds the row; the diagonal entries of the two 512-square diagonal blocks lie between 1 and 2.5.
All inputs are finite; a program needn't handle non-finite values.
Results may differ from a plain program's by a relative error of at most 0.0001.
Values sent between devices are 32-bit elements; how exact they have to be, the bound alone decides.
A program may use at most 64 MiB of HBM per device.

v0:
```python
import jax
import jax.numpy as jnp
from jax import lax
from jax.sharding import PartitionSpec as P

NB = 512


def exact_dot(first, second):
    return jnp.dot(
        first, second, precision=lax.Precision.HIGHEST, preferred_element_type=jnp.float32
    )


def lower_half(matrix):
    return jnp.tril(matrix) - 0.5 * jnp.diag(jnp.diag(matrix))


def local(factor, adjoint):
    row_cycles, tile_rows, col_cycles, tile_cols = factor.shape
    col_devices = lax.axis_size("col")
    row_devices = lax.axis_size("row")
    row_span = tile_rows * row_devices
    col_span = tile_cols * col_devices
    row_index = lax.axis_index("row")
    col_index = lax.axis_index("col")
    local_rows = row_cycles * tile_rows
    local_cols = col_cycles * tile_cols
    left_cols = col_cycles * col_span - 2 * NB
    panel_cycles = 2 * NB // col_span
    row_blocks = 2 * NB // row_span
    owned_rows = row_blocks * tile_rows
    owned_cols = panel_cycles * tile_cols
    split_col = local_cols - owned_cols
    row_steps = jnp.arange(local_rows, dtype=jnp.int32)
    col_steps = jnp.arange(local_cols, dtype=jnp.int32)
    global_rows = row_steps // tile_rows * row_span + row_index * tile_rows + row_steps % tile_rows
    global_cols = col_steps // tile_cols * col_span + col_index * tile_cols + col_steps % tile_cols
    factor_flat = factor.reshape(local_rows, local_cols)
    working = jnp.where(
        global_cols[None, :] - left_cols > global_rows[:, None],
        0.0,
        adjoint.reshape(local_rows, local_cols),
    )
    factor_local = factor_flat[:, split_col:].reshape(local_rows, panel_cycles, tile_cols)
    factor_panels = lax.all_gather(factor_local, "col", axis=2, tiled=True).reshape(
        local_rows, 2 * NB
    )
    factor_tops = factor_flat[:owned_rows].reshape(row_blocks, tile_rows, local_cols)
    diag_part = factor_panels[:owned_rows].reshape(row_blocks, tile_rows, 2 * NB)
    top_rows, diag_full = (
        lax.all_gather(factor_tops, "row", axis=1, tiled=True),
        lax.all_gather(diag_part, "row", axis=1, tiled=True),
    )
    top_rows = top_rows.reshape(2 * NB, local_cols)
    diag_full = diag_full.reshape(2 * NB, 2 * NB)
    owned_global = global_rows[:owned_rows]
    block_ids = jnp.arange(NB, dtype=jnp.int32)
    panel_globals = global_cols[split_col:]
    first_row = NB
    bottom = first_row + NB
    first_col = left_cols + first_row
    beneath = (global_rows >= bottom)[:, None]
    col_left = (global_cols < first_col)[None, :]
    adjoint_local = working[:, split_col:].reshape(local_rows, panel_cycles, tile_cols)
    adjoint_panels = lax.all_gather(adjoint_local, "col", axis=2, tiled=True).reshape(
        local_rows, 2 * NB
    )
    diag_block = diag_full[first_row:bottom, first_row:bottom]
    panel_factor = jnp.where(beneath, factor_panels[:, first_row:bottom], 0.0)
    solved_cols = lax.linalg.triangular_solve(
        diag_block, adjoint_panels[:, first_row:bottom], left_side=False, lower=True
    )
    column_adjoint = jnp.where(beneath, solved_cols, 0.0)
    picker = (owned_global[None, :] == first_row + block_ids[:, None]).astype(jnp.float32)
    partial_sum = exact_dot(picker, adjoint_panels[:owned_rows, first_row:bottom]) - jnp.tril(
        exact_dot(column_adjoint.T, panel_factor)
    )
    diag_start = lax.psum(partial_sum, "row")
    product = lower_half(exact_dot(diag_block.T, diag_start))
    left_solved = lax.linalg.triangular_solve(
        diag_block, product, left_side=True, lower=True, transpose_a=True
    )
    symmetric = lax.linalg.triangular_solve(diag_block, left_solved, left_side=False, lower=True)
    diag_adjoint = lower_half(symmetric + symmetric.T)
    owned_sym = exact_dot(picker.T, diag_adjoint + diag_adjoint.T)
    panel_rows_l = top_rows[first_row:bottom]
    trail_update = exact_dot(column_adjoint, panel_rows_l)
    row_extra = exact_dot(owned_sym, panel_rows_l)
    trail_factor = jnp.where(beneath & col_left, factor_flat, 0.0)
    row_terms = jnp.pad(
        exact_dot(column_adjoint.T, trail_factor), ((first_row, NB - first_row), (0, 0))
    ).reshape(row_blocks, row_span, local_cols)
    summed = lax.psum_scatter(row_terms, "row", scatter_dimension=1, tiled=True).reshape(
        owned_rows, local_cols
    )
    in_panel = ((owned_global >= first_row) & (owned_global < bottom))[:, None]
    row_change = jnp.where(in_panel & col_left, summed + row_extra, 0.0)
    working = working - jnp.where(beneath & col_left, trail_update, 0.0)
    working = jnp.concatenate([working[:owned_rows] - row_change, working[owned_rows:]], 0)
    owned_diag = exact_dot(picker.T, diag_adjoint)
    new_slot = jnp.where(beneath, column_adjoint, adjoint_panels[:, first_row:bottom])
    new_slot = jnp.concatenate(
        [jnp.where(in_panel, owned_diag, new_slot[:owned_rows]), new_slot[owned_rows:]], 0
    )
    new_panels = jnp.concatenate(
        [adjoint_panels[:, :first_row], new_slot, adjoint_panels[:, bottom:]], 1
    )
    local_new = lax.dynamic_index_in_dim(
        new_panels.reshape(local_rows, panel_cycles, col_devices, tile_cols),
        col_index,
        2,
        keepdims=False,
    ).reshape(local_rows, owned_cols)
    in_cols = ((panel_globals >= first_col) & (panel_globals < first_col + NB))[None, :]
    working = jnp.concatenate(
        [working[:, :split_col], jnp.where(in_cols, local_new, working[:, split_col:])], 1
    )
    return working.reshape(row_cycles, tile_rows, col_cycles, tile_cols)


def solution(mesh):
    in_specs = (P(None, "row", None, "col"), P(None, "row", None, "col"))
    out_specs = P(None, "row", None, "col")
    return jax.shard_map(local, mesh=mesh, in_specs=in_specs, out_specs=out_specs, check_vma=False)
```

profile of v0, /device:TPU:0, one launch (start us, length us, event | category | flops | bytes accessed | tf_op | source)
XLA Modules:
  0.0 376.2 jit_solution(3976893358861151109)
XLA Ops:
  6.5 2.7 copy.19
  9.4 1.2 copy-done.4
  10.7 1.4 copy.35
  12.2 40.3 %all-gather.7.cloned.1.call-done = f32[1152,2,512]{0,2,1:T(8,128)} async-done(((f32[1152,2,128]{0,2,1:T(8,128)}), f32[1152,2,512]{0,2,1:T(8,128)}) %all-gather.7.cloned.1.call-update) | async-done | bytes 4718608 | tf_op jit(solution)/shard_map/all_gather | solution.py:46
  52.5 1.9 slice.166
  54.4 1.2 copy.17
  55.9 1.2 copy-done.3
  57.2 1.4 copy.34
  58.7 0.8 copy.38
  59.7 0.6 compare_and_fusion
  60.3 68.9 %all-gather.9.cloned.1.call-done = f32[1,1024,1024]{1,2,0:T(8,128)} async-done(((f32[1,128,1024]{1,2,0:T(8,128)}), f32[1,1024,1024]{1,2,0:T(8,128)}) %all-gather.9.cloned.1.call-update) | async-done | bytes 4194320 | tf_op jit(solution)/shard_map/all_gather | solution.py:53
  129.2 1.3 fusion.19
  130.5 8.9 %while.1 = (s32[]{:T(128)}, f32[512,512]{0,1:T(8,128)S(1)}, s32[4,2]{0,1:T(2,128)S(1)}, f32[4,128,128]{2,1,0:T(8,128)S(1)}, s32[]{:T(128)}) while((s32[]{:T(128)}, f32[512,512]{0,1:T(8,128)S(1)}, s32[4,2]{0,1:T(2,128)S(1)}, f32[4,128,128]{2,1,0:T(8,128)S(1)}, s32[]{:T(128)}) %tuple.22), condition=%wide.while_cond, body=%wide.while_body.sunk | while | flops 2 | bytes 393329 | solution.py:71
  130.6 0.6 fusion.119
  131.2 1.4 dynamic-slice.7
  132.8 0.6 fusion.119
  133.4 1.4 dynamic-slice.7
  135.0 0.6 fusion.119
  135.6 1.4 dynamic-slice.7
  137.3 0.6 fusion.119
  137.8 1.4 dynamic-slice.7
  139.4 39.5 %custom-call.7 = f32[4,128,128]{1,2,0:T(8,128)S(1)} custom-call(f32[4,128,128]{2,1,0:T(8,128)S(1)} %get-tuple-element.12), custom_call_target="InvertDiagBlocksLowerTriangular" | custom-call | tf_op jit(solution)/shard_map/triangular_solve | solution.py:71
  178.9 1.9 fusion.34
  180.8 1.7 convolution_subtract_fusion.2
  182.5 0.7 fusion.63
  183.2 2.0 convolution_subtract_fusion.1
  185.2 0.7 fusion.66
  185.9 2.5 convolution_subtract_fusion
  188.3 1.5 fusion.69
  189.9 4.4 %fusion.9 = f32[512,512]{0,1:T(8,128)S(1)} fusion(f32[1152,1024]{0,1:T(8,128)S(1)} %bitcast.101, pred[1152]{0:T(1024)(128)(4,1)S(1)} %broadcast_compare_fusion, f32[1152,128]{0,1:T(8,128)S(1)} %fusion.34, f32[1152,128]{0,1:T(8,128)S(1)} %fusion.63, f32[1152,128]{0,1:T(8,128)S(1)} %fusion.66, f32[1152,128]{0,1:T(8,128)S(1)} %fusion.69), kind=kOutput, calls=%fused_computation.29 | convolution fusion | flops 3627352064 | bytes 5771264 | tf_op jit(solution)/shard_map/dot_general | solution.py:10
  194.3 2.7 convolution_subtract_fusion.3
  197.3 4.4 %fusion.102 = (f32[1152,512]{0,1:T(8,128)}, f32[1152,512]{0,1:T(8,128)S(1)}) fusion(f32[1152,1024]{0,1:T(8,128)} %bitcast.86, f32[1152,128]{0,1:T(8,128)S(1)} %fusion.34, f32[1152,128]{0,1:T(8,128)S(1)} %fusion.63, f32[1152,128]{0,1:T(8,128)S(1)} %fusion.66, f32[1152,128]{0,1:T(8,128)S(1)} %fusion.69, pred[1152]{0:T(1024)(128)(4,1)S(1)} %broadcast_compare_fusion), kind=kLoop, calls=%fused_computation.162 | loop fusion | flops 2949120 | bytes 11797632 | tf_op jit(solution)/shard_map/slice | solution.py:107
  201.7 1.5 copy-done.1
  203.2 1.6 slice.177
  204.8 8.0 %all-gather.11.cloned.1.call-done = f32[1,1024,384]{1,2,0:T(8,128)} async-done(((f32[1,128,384]{1,2,0:T(8,128)}), f32[1,1024,384]{1,2,0:T(8,128)}) %all-gather.11.cloned.1.call-update) | async-done | bytes 1572880 | tf_op jit(solution)/shard_map/all_gather | solution.py:52
  212.8 9.6 %fusion = f32[1152,384]{1,0:T(8,128)S(1)} fusion(f32[1152,384]{1,0:T(8,128)} %copy-done.3, pred[384]{0:T(512)(128)(4,1)S(1)} %broadcast_compare_fusion.1, pred[1152]{0:T(1024)(128)(4,1)S(1)} %broadcast_compare_fusion, f32[1,1024,384]{1,2,0:T(8,128)} %all-gather.11.cloned.1.call-done, f32[1152,128]{0,1:T(8,128)S(1)} %fusion.34, f32[1152,128]{0,1:T(8,128)S(1)} %fusion.63, ...), kind=kOutput, calls=%fused_computation.6 | convolution fusion | flops 2721595392 | bytes 6689280 | tf_op jit(solution)/shard_map/dot_general | solution.py:10
  222.5 1.2 slice.173
  223.7 1.4 copy-done.5
  225.1 4.9 %fusion.2 = f32[512,384]{1,0:T(8,128)S(1)} fusion(f32[1152,384]{1,0:T(8,128)S(1)} %bitcast.91, pred[384]{0:T(512)(128)(4,1)S(1)} %broadcast_compare_fusion.1, pred[1152]{0:T(1024)(128)(4,1)S(1)} %broadcast_compare_fusion, f32[1152,128]{0,1:T(8,128)S(1)} %fusion.34, f32[1152,128]{0,1:T(8,128)S(1)} %fusion.63, f32[1152,128]{0,1:T(8,128)S(1)} %fusion.66, ...), kind=kOutput, calls=%fused_computation.15 | convolution fusion | flops 2721153024 | bytes 4916736 | tf_op jit(solution)/shard_map/dot_general | solution.py:10
  230.1 1.3 pad_bitcast_fusion
  231.4 61.4 %all-reduce.3.cloned.1.call-done = f32[512,512]{0,1:T(8,128)} async-done(((f32[512,512]{0,1:T(8,128)}), f32[512,512]{0,1:T(8,128)}) %all-reduce.3.cloned.1.call-update) | async-done | bytes 1048592 | tf_op jit(solution)/shard_map/psum | solution.py:79
  292.8 3.4 convolution_bitcast_fusion
  296.2 4.5 %gather_fusion = f32[512]{0:T(512)S(1)} fusion(f32[512,512]{0,1:T(8,128)S(1)} %convolution_bitcast_fusion, s32[512]{0:T(512)S(1)} %bitcast.79), kind=kCustom, calls=%fused_computation | custom fusion | bytes 8192 | tf_op jit(solution)/shard_map/jit(_diag)/jit(diagonal)/cond/branch_0_fun/gather | solution.py:16
  301.3 0.6 convolution_subtract_fusion.7
  302.3 1.0 convolution_subtract_fusion.6
  303.7 1.5 convolution_subtract_fusion.9
  305.6 0.4 fusion.44
  306.1 0.6 convolution_subtract_fusion.5
  307.1 0.9 copy.25
  308.0 1.0 convolution_subtract_fusion.4
  309.4 0.8 copy.24
  310.2 1.5 convolution_subtract_fusion.8
  312.2 1.1 pad_maximum_fusion.2
  313.7 1.1 bitcast_add_fusion.2
  314.8 4.7 %gather_fusion.1 = f32[512]{0:T(512)S(1)} fusion(f32[512,512]{0,1:T(8,128)S(1)} %bitcast_add_fusion.2, s32[512]{0:T(512)S(1)} %bitcast.80), kind=kCustom, calls=%fused_computation.1 | custom fusion | bytes 8192 | tf_op jit(solution)/shard_map/jit(_diag)/jit(diagonal)/cond/branch_0_fun/gather | solution.py:16
  319.6 1.3 copy.28
  321.0 1.6 convolution_select_fusion.1
  322.6 1.9 maximum_maximum_fusion
  325.0 2.1 fusion.18
  327.1 34.3 %reduce-scatter.2.cloned.1.call-done = f32[1,128,384]{2,1,0:T(8,128)} async-done(((f32[1,1024,384]{2,1,0:T(8,128)}), f32[1,128,384]{2,1,0:T(8,128)}) %reduce-scatter.2.cloned.1.call-update) | async-done | bytes 196624 | tf_op jit(solution)/shard_map/reduce_scatter | solution.py:94
  361.5 2.1 fusion.17
  363.8 1.3 fusion.3
  365.1 2.7 reshape.150
  367.8 1.4 copy.31
  (91 shorter events, 6.0 us)
Async XLA Ops:
  6.5 45.9 %all-gather.7.cloned.1.call-start = ((), (), s32[]{:S(2)}) async-start(), calls=%async_computation.2 | async-start | bytes 5898240 | tf_op jit(solution)/shard_map/all_gather | solution.py:46
  9.4 1.2 copy-start.4
  10.7 43.7 %copy-start.12 = (f32[9,128,3,128]{3,1,2,0:T(8,128)S(1)}, f32[9,128,3,128]{3,1,2,0:T(8,128)}, u32[]{:S(2)}) copy-start(f32[9,128,3,128]{3,1,2,0:T(8,128)} %param.3) | copy-start | bytes 5308420
  12.1 117.0 %all-gather.9.cloned.1.call-start = ((), (), s32[]{:S(2)}) async-start(), calls=%async_computation.3 | async-start | bytes 4718592 | tf_op jit(solution)/shard_map/all_gather | solution.py:53
  54.3 124.6 %all-gather.5.cloned.1.call-start = ((), (), s32[]{:S(2)}) async-start(), calls=%async_computation.1 | async-start | bytes 5898240 | tf_op jit(solution)/shard_map/all_gather | solution.py:66
  55.9 1.2 copy-start.3
  57.2 1.5 slice-start
  58.7 154.2 %all-gather.11.cloned.1.call-start = ((), (), s32[]{:S(2)}) async-start(), calls=%async_computation.4 | async-start | bytes 1769472 | tf_op jit(solution)/shard_map/all_gather | solution.py:52
  59.6 233.2 %all-reduce.3.cloned.1.call-start = ((), (), s32[]{:S(2)}) async-start(), calls=%async_computation.6 | async-start | bytes 2097152 | tf_op jit(solution)/shard_map/psum | solution.py:79
  59.6 164.1 %copy-start.13 = (pred[384]{0:T(512)(128)(4,1)}, pred[384]{0:T(512)(128)(4,1)S(1)}, u32[]{:S(2)}) copy-start(pred[384]{0:T(512)(128)(4,1)S(1)} %broadcast_compare_fusion.1) | copy-start | bytes 1156
  178.9 6.3 %copy-start.6 = (f32[4,128,128]{1,2,0:T(8,128)}, f32[4,128,128]{1,2,0:T(8,128)S(1)}, u32[]{:S(2)}) copy-start(f32[4,128,128]{1,2,0:T(8,128)S(1)} %custom-call.7) | copy-start | bytes 786436
  178.9 10.9 %slice-start.1 = ((s8[4718592]{0:T(1024)(128)(4,1)}), s8[4194304]{0:T(1024)(128)(4,1)S(1)}, s32[]{:S(2)}) async-start(s8[4718592]{0:T(1024)(128)(4,1)} %bitcast.99), calls=%async_computation.8 | async-start | bytes 8388608
  183.2 6.6 %slice-start.2 = ((s8[4718592]{0:T(1024)(128)(4,1)}), s8[524288]{0:T(1024)(128)(4,1)S(1)}, s32[]{:S(2)}) async-start(s8[4718592]{0:T(1024)(128)(4,1)} %bitcast.99), calls=%async_computation.9 | async-start | bytes 1048576
  197.0 164.5 %reduce-scatter.2.cloned.1.call-start = ((), (), s32[]{:S(2)}) async-start(), calls=%async_computation.5 | async-start | bytes 1769472 | tf_op jit(solution)/shard_map/reduce_scatter | solution.py:94
  201.7 1.5 copy-start.1
  222.4 7.6 %copy-start.11 = (f32[1152,384]{1,0:T(8,128)}, f32[1152,384]{1,0:T(8,128)S(1)}, u32[]{:S(2)}) copy-start(f32[1152,384]{1,0:T(8,128)S(1)} %fusion) | copy-start | bytes 5308420
  222.4 2.7 copy-start.5
  296.2 4.7 %copy-start.7 = (f32[4,128,128]{1,2,0:T(8,128)S(1)}, f32[4,128,128]{1,2,0:T(8,128)}, u32[]{:S(2)}) copy-start(f32[4,128,128]{1,2,0:T(8,128)} %copy-done.6) | copy-start | bytes 786436
  306.1 6.0 %copy-start.8 = (f32[512,128]{1,0:T(8,128)}, f32[512,128]{1,0:T(8,128)S(1)}, u32[]{:S(2)}) copy-start(f32[512,128]{1,0:T(8,128)S(1)} %copy.26) | copy-start | bytes 786436
  311.7 1.9 copy-start.9
  311.7 1.9 copy-start.10
  319.6 3.0 copy-start.2
  324.6 36.9 %copy-start.14 = (pred[384]{0:T(512)(128)(4,1)S(1)}, pred[384]{0:T(512)(128)(4,1)}, u32[]{:S(2)}) copy-start(pred[384]{0:T(512)(128)(4,1)} %copy-done.13) | copy-start | bytes 1156
  325.0 38.6 %copy-start.15 = (pred[256]{0:T(512)(128)(4,1)S(1)}, pred[256]{0:T(512)(128)(4,1)}, u32[]{:S(2)}) copy-start(pred[256]{0:T(512)(128)(4,1)} %compare_and_fusion) | copy-start | bytes 772
  327.1 36.5 %copy-start = (f32[1024,384]{1,0:T(8,128)S(1)}, f32[1024,384]{1,0:T(8,128)}, u32[]{:S(2)}) copy-start(f32[1024,384]{1,0:T(8,128)} %slice.173) | copy-start | bytes 4718596
Sparse Core Ops, SparseCore 0:
  12.3 40.1 all-gather.6
  54.5 74.6 all-gather.8
  130.7 35.6 all-gather.4
  168.3 44.4 all-gather.10
  216.2 76.5 all-reduce.2
  296.1 65.3 reduce-scatter.1
where the time goes:
time: 382 us; the launch traced here: 376 us
  waiting for transfers between devices  213 us (56%)
  other arithmetic  52.1 us (14%)
  matrix products  50.9 us (13%)
  local copies, waits for them, and re-layouts  45.3 us (12%)
  between operations  14.4 us (4%)
    all_gather x1, waiting for transfers between devices, local(): lax.all_gather(diag_part, 'row', axis=1, tiled=True)  68.9 us
    psum x1, waiting for transfers between devices, local(): diag_start = lax.psum(partial_sum, 'row')  61.4 us
    another operation x3, other arithmetic, local(): lax.linalg.triangular_solve(diag_block, adjoint_panels[:, first_row:botto...  40.8 us
    all_gather x1, waiting for transfers between devices, local(): lax.all_gather(factor_local, 'col', axis=2, tiled=True)  40.3 us
    reduce_scatter x1, waiting for transfers between devices, local(): lax.psum_scatter(row_terms, 'row', scatter_dimension=1, tiled=True)  34.3 us
    dot_general x8, matrix products, exact_dot(): jnp.dot(first, second, precision=lax.Precision.HIGHEST, preferred_element...  30.9 us
    another operation x7, matrix products, local(): lax.linalg.triangular_solve(diag_block, adjoint_panels[:, first_row:botto...  10.8 us
    unnamed x40, local copies, waits for them, and re-layouts  10.3 us
  transfers between devices with their start and end apart: 6, of which 5 were waited for; matrix products, arithmetic and copies ran while one was open for 34% of the time, Pallas kernels for 0%

commit v1 on v0

v1 whole, which is shorter than its diff:
```python
import functools

import jax
import jax.numpy as jnp
from jax import lax
from jax.experimental import pallas as pl
from jax.experimental.pallas import tpu as pltpu
from jax.sharding import PartitionSpec as P

NB = 512
LANES = 128
MESH = pl.DeviceIdType.MESH


def dot(first, second, first_dim=1):
    return lax.dot_general(
        first,
        second,
        (((first_dim,), (0,)), ((), ())),
        precision=lax.Precision.HIGHEST,
        preferred_element_type=jnp.float32,
    )


def iota(shape, dim):
    return lax.broadcasted_iota(jnp.int32, shape, dim)


class Plan:
    def __init__(self, rows, cols, shape):
        self.rows, self.cols = rows, cols
        self.cycles, self.col_cycles, self.tile, _ = shape
        self.nx = 1
        while 2 * (2 * self.nx) ** 2 <= rows:
            self.nx *= 2
        self.nz = rows // self.nx
        self.owners = NB // self.tile
        self.owner_z = self.owners // self.nx
        self.panels = NB // LANES
        self.ny = cols // 2
        self.left = self.col_cycles * cols * LANES - 2 * NB


class ColumnGather:
    def __init__(self, plan, col, full, send, pair, forward, recv):
        self.plan, self.col, self.full = plan, col, full
        self.send, self.pair, self.forward, self.recv = send, pair, forward, recv
        self.first = plan.cols - plan.panels
        self.y, self.core = col // 2, col % 2
        self.mine = col - self.first

    def slot(self, block):
        return self.full.at[:, :, pl.ds(pl.multiple_of(block * LANES, LANES), LANES)]

    def copy(self, src, block, send, col):
        return pltpu.make_async_remote_copy(
            src_ref=src,
            dst_ref=self.slot(block),
            send_sem=send,
            recv_sem=self.recv.at[block],
            device_id={"col": col},
            device_id_type=MESH,
        )

    def other(self, step):
        return (self.y + step) % self.plan.ny

    def copies(self, src):
        out = [
            self.copy(src, self.mine, self.send.at[step], self.other(step) * 2 + self.core)
            for step in range(1, self.plan.ny)
        ]
        out.append(self.copy(src, self.mine, self.pair, self.y * 2 + 1 - self.core))
        return out

    def own(self, src):
        return pltpu.make_async_copy(src, self.slot(self.mine), self.recv.at[self.mine])

    def start(self, src):
        @pl.when(self.mine >= 0)
        def _():
            for copy in self.copies(src):
                copy.start()
            self.own(src).start()

    def relay(self):
        for step in range(1, self.plan.ny):
            block = self.other(step) * 2 + self.core - self.first

            @pl.when(block >= 0)
            def _():
                copy = self.copy(
                    self.slot(block), block, self.forward.at[step], self.y * 2 + 1 - self.core
                )
                copy.wait_recv()
                copy.start()

    def finish(self, src):
        @pl.when(self.mine >= 0)
        def _():
            self.own(src).wait()

        for step in range(self.plan.ny):
            block = self.other(step) * 2 + 1 - self.core - self.first

            @pl.when(block >= 0)
            def _():
                self.copy(self.slot(block), block, self.pair, self.y * 2 + 1 - self.core).wait_recv()

    def drain(self, src):
        @pl.when(self.mine >= 0)
        def _():
            for copy in self.copies(src):
                copy.wait_send()

        for step in range(1, self.plan.ny):
            block = self.other(step) * 2 + self.core - self.first

            @pl.when(block >= 0)
            def _():
                self.copy(
                    self.slot(block), block, self.forward.at[step], self.y * 2 + 1 - self.core
                ).wait_send()


def invert(full, inverse):
    row, col = iota((LANES, LANES), 0), iota((LANES, LANES), 1)
    count = NB // LANES
    blocks = []
    for k in range(count):
        part = full[k * LANES : (k + 1) * LANES, k * LANES : (k + 1) * LANES]
        blocks.append((part, jnp.where(row == col, 1.0 / jnp.where(row == col, part, 1.0), 0.0)))
    size = 1
    while size < LANES:
        mask = (
            (row // (2 * size) == col // (2 * size))
            & (row // size % 2 == 1)
            & (col // size % 2 == 0)
        )
        half = [dot(jnp.where(mask, part, 0.0), inv) for part, inv in blocks]
        blocks = [(part, inv - dot(inv, other)) for (part, inv), other in zip(blocks, half)]
        size *= 2
    inverse[...] = jnp.zeros_like(inverse)
    for k in range(count):
        inverse[k * LANES : (k + 1) * LANES, k * LANES : (k + 1) * LANES] = blocks[k][1]
    while size < NB:
        for base in range(0, NB, 2 * size):
            top, low = slice(base, base + size), slice(base + size, base + 2 * size)
            inner = dot(full[low, top], inverse[top, top])
            inverse[low, top] = -dot(inverse[low, low], inner)
        size *= 2


def kernel(
    plan, factor, adjoint, out,
    panel, top, diag, inv, inv_t, corner, spread, yval, ysum, xrecv, zrecv, starts, start_full,
    a_send, a_pair, a_fwd, a_recv, d_send, d_pair, d_fwd, d_recv,
    s_send, s_pair, s_fwd, s_recv,
    t_z, t_x, t_fwd, t_recv, x_send, x_recv, z_send, z_recv, r_send, r_recv,
):
    p = plan
    row, col = lax.axis_index("row"), lax.axis_index("col")
    z, x = row // p.nx, row % p.nx
    last = p.col_cycles - 1
    tile, depth = p.tile, (p.cycles - 1) * p.tile
    width = p.col_cycles * LANES
    owner = row - (p.rows - p.owners)
    first_z = p.nz - p.owner_z
    is_panel = col >= p.cols - p.panels
    mine = col - (p.cols - p.panels)
    order = [last] + list(range(last))

    barrier = pltpu.get_barrier_semaphore()
    for step in range(1, p.rows):
        pl.semaphore_signal(
            barrier, inc=1, device_id={"row": (row + step) % p.rows}, device_id_type=MESH
        )
    for step in range(1, p.cols):
        pl.semaphore_signal(
            barrier, inc=1, device_id={"col": (col + step) % p.cols}, device_id_type=MESH
        )
    pl.semaphore_wait(barrier, p.rows + p.cols - 2)

    def to_row(src, dst, send, recv, target):
        return pltpu.make_async_remote_copy(
            src_ref=src, dst_ref=dst, send_sem=send, recv_sem=recv,
            device_id={"row": target}, device_id_type=MESH,
        )

    gather_a = ColumnGather(p, col, panel, a_send, a_pair, a_fwd, a_recv)
    a_src = adjoint.at[1:, last]
    gather_a.start(a_src)

    def top_slot(index, e):
        return top.at[index, :, e * LANES : (e + 1) * LANES]

    def top_copies(e):
        src = factor.at[0, e]
        dst, recv = top_slot(owner, e), t_recv.at[e, owner]
        made = [
            to_row(src, dst, t_z.at[e, k], recv, (z + k) % p.nz * p.nx + x) for k in range(1, p.nz)
        ]
        return made + [
            to_row(src, dst, t_x.at[e, k], recv, z * p.nx + (x + k) % p.nx) for k in range(1, p.nx)
        ]

    def top_own(e):
        return pltpu.make_async_copy(factor.at[0, e], top_slot(owner, e), t_recv.at[e, owner])

    @pl.when(owner >= 0)
    def _():
        for e in order:
            for copy in top_copies(e):
                copy.start()
            top_own(e).start()

    def top_forward(e, zi, action):
        index = zi * p.nx + x

        @pl.when(z != first_z + zi)
        def _():
            slot = top_slot(index, e)
            for k in range(1, p.nx):
                copy = to_row(
                    slot, slot, t_fwd.at[e, zi, k], t_recv.at[e, index],
                    z * p.nx + (x + k) % p.nx,
                )
                action(copy, k)

    def relay(copy, k):
        if k == 1:
            copy.wait_recv()
        copy.start()

    def top_relay(e):
        for zi in range(p.owner_z):
            top_forward(e, zi, relay)

    def top_finish(e):
        @pl.when(owner >= 0)
        def _():
            top_own(e).wait()

        for zi in range(p.owner_z):
            for k in range(1, p.nx):
                index = zi * p.nx + (x + k) % p.nx
                slot = top_slot(index, e)
                to_row(slot, slot, t_x.at[e, k], t_recv.at[e, index], row).wait_recv()

    top_relay(last)
    top_finish(last)
    gather_d = ColumnGather(p, col, diag, d_send, d_pair, d_fwd, d_recv)
    d_src = top.at[:, :, last * LANES : width]
    gather_d.start(d_src)
    gather_a.relay()
    for e in range(last):
        top_relay(e)
    gather_d.relay()
    gather_a.finish(a_src)

    a_full = panel[...].reshape(depth, NB)
    columns = [factor[1:, e].reshape(depth, LANES) for e in range(p.col_cycles)]
    corner[...] = dot(a_full, jnp.concatenate(columns, 1), 0)

    gather_d.finish(d_src)
    full = diag.reshape(NB, NB)
    invert(full, inv)
    inv_t[...] = inv[...].T.reshape(inv_t.shape)

    def x_copy(e, k):
        target = (x + k) % p.nx
        return to_row(
            yval.at[e, target], xrecv.at[e, x], x_send.at[e, k], x_recv.at[e, x],
            z * p.nx + target,
        )

    inv_tv = inv_t[...].reshape(NB, NB)

    def put(e, value):
        value = value.reshape(p.owner_z, p.nx, tile, LANES)
        for k in range(p.nx):
            yval[e, k] = value[:, k]
        for k in range(1, p.nx):
            x_copy(e, k).start()

    put(last, dot(inv_tv, corner[:, last * LANES : width]))
    rest = dot(inv_tv, corner[:, : last * LANES])
    for e in range(last):
        put(e, rest[:, e * LANES : (e + 1) * LANES])

    def z_copy(e, zi):
        return to_row(
            ysum.at[e, zi], zrecv.at[e, z], z_send.at[e, zi], z_recv.at[e, z],
            (first_z + zi) * p.nx + x,
        )

    def x_sum(e):
        total = yval[e, x]
        for k in range(1, p.nx):
            source = (x + k) % p.nx
            to_row(
                xrecv.at[e, source], xrecv.at[e, source], x_send.at[e, k], x_recv.at[e, source], row
            ).wait_recv()
            total = total + xrecv[e, source]
        ysum[e] = total
        for zi in range(p.owner_z):
            @pl.when(z != first_z + zi)
            def _():
                z_copy(e, zi).start()

    x_sum(last)
    for e in range(last):
        top_finish(e)
    rights = top[...].reshape(NB, width)
    unit = (iota((NB, LANES), 0) == mine * LANES + iota((NB, LANES), 1)).astype(jnp.float32)
    rights = jnp.concatenate(
        [rights[:, : last * LANES], jnp.where(is_panel, unit, rights[:, last * LANES :])], 1
    )
    spread[...] = dot(inv[...], rights)
    for e in range(last):
        x_sum(e)

    def trail(begin, end):
        change = dot(panel[begin:end].reshape((end - begin) * tile, NB), spread[...])
        change = change.reshape(end - begin, tile, width)
        for e in range(p.col_cycles):
            part = change[:, :, e * LANES : (e + 1) * LANES]
            moved = adjoint[1 + begin : 1 + end, e] - part
            if e == last:
                moved = jnp.where(is_panel, part, moved)
            out[1 + begin : 1 + end, e] = moved

    middle = (p.cycles - 1) // 2
    trail(0, middle)

    def z_sum(e):
        total = ysum[e, owner // p.nx]
        for k in range(1, p.nz):
            source = (z + k) % p.nz
            to_row(
                zrecv.at[e, source], zrecv.at[e, source], z_send.at[e, 0], z_recv.at[e, source], row
            ).wait_recv()
            total = total + zrecv[e, source]
        return total

    def start_copies():
        first = p.rows - p.owners
        return [
            to_row(
                starts.at[owner], starts.at[owner], r_send.at[k], r_recv.at[owner],
                first + (owner + k) % p.owners,
            )
            for k in range(1, p.owners)
        ]

    lower = iota((tile, LANES), 0) + owner * tile >= iota((tile, LANES), 1) + mine * LANES
    gather_s = ColumnGather(p, col, start_full, s_send, s_pair, s_fwd, s_recv)

    @pl.when((owner >= 0) & is_panel)
    def _():
        starts[owner] = jnp.where(lower, adjoint[0, last] - z_sum(last), 0.0)
        for copy in start_copies():
            copy.start()

    trail(middle, p.cycles - 1)

    @pl.when(owner < 0)
    def _():
        for e in range(p.col_cycles):
            rows_at = iota((tile, LANES), 0) + row * tile
            cols_at = iota((tile, LANES), 1) + (e * p.cols + col) * LANES - p.left
            out[0, e] = jnp.where(cols_at > rows_at, 0.0, adjoint[0, e])

    @pl.when(owner >= 0)
    def _():
        @pl.when(is_panel)
        def _():
            for k in range(1, p.owners):
                source = (owner + k) % p.owners
                to_row(
                    starts.at[source], starts.at[source], r_send.at[k], r_recv.at[source], row
                ).wait_recv()

        gather_s.start(starts)
        gather_s.relay()
        gather_s.finish(starts)
        product = dot(full[...], start_full[...].reshape(NB, NB), 0)
        row_at, col_at = iota((NB, NB), 0), iota((NB, NB), 1)
        both = (
            jnp.where(row_at >= col_at, product, 0.0) + jnp.where(row_at > col_at, product, 0.0).T
        )
        changes = dot(dot(inv_t[owner], both), spread[...])
        for e in range(last):
            out[0, e] = adjoint[0, e] - z_sum(e) - changes[:, e * LANES : (e + 1) * LANES]

        part = changes[:, last * LANES :]

        @pl.when(is_panel)
        def _():
            equal = iota((tile, LANES), 0) + owner * tile == iota((tile, LANES), 1) + mine * LANES
            out[0, last] = jnp.where(lower, jnp.where(equal, 0.5 * part, part), 0.0)

        @pl.when(jnp.logical_not(is_panel))
        def _():
            out[0, last] = adjoint[0, last] - z_sum(last) - part

        gather_s.drain(starts)

        @pl.when(is_panel)
        def _():
            for copy in start_copies():
                copy.wait_send()

    gather_a.drain(a_src)
    gather_d.drain(d_src)
    for e in order:
        @pl.when(owner >= 0)
        def _():
            for copy in top_copies(e):
                copy.wait_send()

        for zi in range(p.owner_z):
            top_forward(e, zi, lambda copy, k: copy.wait_send())

            @pl.when(z != first_z + zi)
            def _():
                z_copy(e, zi).wait_send()

        for k in range(1, p.nx):
            x_copy(e, k).wait_send()


def local(rows, cols, factor, adjoint):
    factor = jnp.transpose(factor, (0, 2, 1, 3))
    adjoint = jnp.transpose(adjoint, (0, 2, 1, 3))
    p = Plan(rows, cols, factor.shape)
    n, cc, tile = p.cycles - 1, p.col_cycles, p.tile
    dma = pltpu.SemaphoreType.DMA
    column = [dma((p.ny,)), dma, dma((p.ny,)), dma((p.panels,))]
    vmem = lambda *shape: pltpu.VMEM(shape, jnp.float32)
    result = pl.pallas_call(
        functools.partial(kernel, p),
        out_shape=jax.ShapeDtypeStruct(factor.shape, jnp.float32),
        in_specs=[pl.BlockSpec(memory_space=pltpu.VMEM)] * 2,
        out_specs=pl.BlockSpec(memory_space=pltpu.VMEM),
        scratch_shapes=[
            vmem(n, tile, NB),
            vmem(p.owners, tile, cc * LANES),
            vmem(p.owners, tile, NB),
            vmem(NB, NB),
            vmem(p.owners, tile, NB),
            vmem(NB, cc * LANES),
            vmem(NB, cc * LANES),
            vmem(cc, p.nx, p.owner_z, tile, LANES),
            vmem(cc, p.owner_z, tile, LANES),
            vmem(cc, p.nx, p.owner_z, tile, LANES),
            vmem(cc, p.nz, tile, LANES),
            vmem(p.owners, tile, LANES),
            vmem(p.owners, tile, NB),
            *column, *column, *column,
            dma((cc, p.nz)), dma((cc, p.nx)), dma((cc, p.owner_z, p.nx)), dma((cc, p.owners)),
            dma((cc, p.nx)), dma((cc, p.nx)), dma((cc, p.owner_z)), dma((cc, p.nz)),
            dma((p.owners,)), dma((p.owners,)),
        ],
        compiler_params=pltpu.CompilerParams(
            collective_id=0, has_side_effects=True, vmem_limit_bytes=48 * 1024 * 1024
        ),
    )(factor, adjoint)
    return jnp.transpose(result, (0, 2, 1, 3))


def solution(mesh):
    spec = P(None, "row", None, "col")
    step = functools.partial(local, mesh.shape["row"], mesh.shape["col"])
    return jax.shard_map(
        step, mesh=mesh, in_specs=(spec, spec), out_specs=spec, check_vma=False
    )
```

time: 382 us -> 68.8 us (0.18)
  the two profiles are of different devices: /device:TPU:0 before, /device:TPU:19 now
where the time goes in v1:
time: 68.8 us; the launch traced here: 68.4 us
  Pallas kernels  64.3 us (93%)
  local copies, waits for them, and re-layouts  4.16 us (6%)
    pallas_call x1, Pallas kernels, local(): pl.pallas_call(functools.partial(kernel, p), out_shape=jax.ShapeDtypeStru...  64.3 us
    unnamed x5, local copies, waits for them, and re-layouts  4.16 us

profile of v1, /device:TPU:19, one launch (start us, length us, event | category | flops | bytes accessed | tf_op | source)
XLA Modules:
  0.0 68.4 jit_solution(11699682283678696779)
XLA Ops:
  0.0 0.0 copy-start
  0.0 1.5 %copy-done = f32[9,128,3,128]{3,1,2,0:T(8,128)S(1)} copy-done((f32[9,128,3,128]{3,1,2,0:T(8,128)S(1)}, f32[9,128,3,128]{3,1,2,0:T(8,128)}, u32[]{:S(2)}) %copy-start) | copy-done | bytes 1769496
  1.5 0.0 copy-start.1
  1.5 1.5 %copy-done.1 = f32[9,128,3,128]{3,1,2,0:T(8,128)S(1)} copy-done((f32[9,128,3,128]{3,1,2,0:T(8,128)S(1)}, f32[9,128,3,128]{3,1,2,0:T(8,128)}, u32[]{:S(2)}) %copy-start.1) | copy-done | bytes 1769496
  3.0 64.3 %shard_map.28 = f32[9,3,128,128]{3,2,1,0:T(8,128)S(1)} custom-call(f32[9,3,128,128]{3,2,1,0:T(8,128)S(1)} %bitcast.4, f32[9,3,128,128]{3,2,1,0:T(8,128)S(1)} %bitcast.5), custom_call_target="tpu_custom_call" | custom-call | tf_op jit(solution)/shard_map/pallas_call | solution.py:441
  67.2 1.2 %copy.4 = f32[9,128,3,128]{3,1,2,0:T(8,128)} copy(f32[9,128,3,128]{3,1,2,0:T(8,128)S(1)} %bitcast.3) | data formatting | bytes 3538944
Async XLA Ops:
  0.0 1.5 %copy-start = (f32[9,128,3,128]{3,1,2,0:T(8,128)S(1)}, f32[9,128,3,128]{3,1,2,0:T(8,128)}, u32[]{:S(2)}) copy-start(f32[9,128,3,128]{3,1,2,0:T(8,128)} %param.2) | copy-start | bytes 5308420
  1.5 1.5 %copy-start.1 = (f32[9,128,3,128]{3,1,2,0:T(8,128)S(1)}, f32[9,128,3,128]{3,1,2,0:T(8,128)}, u32[]{:S(2)}) copy-start(f32[9,128,3,128]{3,1,2,0:T(8,128)} %param.3) | copy-start | bytes 5308420

commit v2 on v1

--- a/solution.py
+++ b/solution.py
@@ -20,6 +20,25 @@
         precision=lax.Precision.HIGHEST,
         preferred_element_type=jnp.float32,
     )
+
+
+def halves(value):
+    high = value.astype(jnp.bfloat16)
+    return high, (value - high.astype(jnp.float32)).astype(jnp.bfloat16)
+
+
+def dot3(first, second, first_dim=1):
+    if not isinstance(first, tuple):
+        first = halves(first)
+    if not isinstance(second, tuple):
+        second = halves(second)
+
+    def one(a, b):
+        return lax.dot_general(
+            a, b, (((first_dim,), (0,)), ((), ())), preferred_element_type=jnp.float32
+        )
+
+    return one(first[0], second[0]) + (one(first[0], second[1]) + one(first[1], second[0]))
 
 
 def iota(shape, dim):
@@ -152,9 +171,9 @@
 
 
 def kernel(
-    plan, factor, adjoint, out,
+    plan, factor_in, adjoint_in, out, factor, adjoint, in_sems,
     panel, top, diag, inv, inv_t, corner, spread, yval, ysum, xrecv, zrecv, starts, start_full,
-    a_send, a_pair, a_fwd, a_recv, d_send, d_pair, d_fwd, d_recv,
+    a_send, a_pair, a_fwd, a_recv, b_send, b_pair, b_fwd, b_recv, d_send, d_pair, d_fwd, d_recv,
     s_send, s_pair, s_fwd, s_recv,
     t_z, t_x, t_fwd, t_recv, x_send, x_recv, z_send, z_recv, r_send, r_recv,
 ):
@@ -170,6 +189,10 @@
     mine = col - (p.cols - p.panels)
     order = [last] + list(range(last))
 
+    load_factor = pltpu.make_async_copy(factor_in, factor, in_sems.at[0])
+    load_adjoint = pltpu.make_async_copy(adjoint_in, adjoint, in_sems.at[1])
+    load_factor.start()
+    load_adjoint.start()
     barrier = pltpu.get_barrier_semaphore()
     for step in range(1, p.rows):
         pl.semaphore_signal(
@@ -187,9 +210,7 @@
             device_id={"row": target}, device_id_type=MESH,
         )
 
-    gather_a = ColumnGather(p, col, panel, a_send, a_pair, a_fwd, a_recv)
-    a_src = adjoint.at[1:, last]
-    gather_a.start(a_src)
+    load_factor.wait()
 
     def top_slot(index, e):
         return top.at[index, :, e * LANES : (e + 1) * LANES]
@@ -214,6 +235,13 @@
                 copy.start()
             top_own(e).start()
 
+    load_adjoint.wait()
+    cut = (p.cycles - 1) * 3 // 4
+    gather_a = ColumnGather(p, col, panel.at[:cut], a_send, a_pair, a_fwd, a_recv)
+    gather_b = ColumnGather(p, col, panel.at[cut:], b_send, b_pair, b_fwd, b_recv)
+    a_src, b_src = adjoint.at[1 : 1 + cut, last], adjoint.at[1 + cut :, last]
+    gather_a.start(a_src)
+
     def top_forward(e, zi, action):
         index = zi * p.nx + x
 
@@ -252,20 +280,28 @@
     gather_d = ColumnGather(p, col, diag, d_send, d_pair, d_fwd, d_recv)
     d_src = top.at[:, :, last * LANES : width]
     gather_d.start(d_src)
+    gather_b.start(b_src)
     gather_a.relay()
     for e in range(last):
         top_relay(e)
+    gather_a.finish(a_src)
+
+    def corner_part(begin, end):
+        rows_of = (end - begin) * tile
+        columns = [
+            factor[1 + begin : 1 + end, e].reshape(rows_of, LANES) for e in range(p.col_cycles)
+        ]
+        return dot3(panel[begin:end].reshape(rows_of, NB), jnp.concatenate(columns, 1), 0)
+
+    corner[...] = corner_part(0, cut)
     gather_d.relay()
-    gather_a.finish(a_src)
-
-    a_full = panel[...].reshape(depth, NB)
-    columns = [factor[1:, e].reshape(depth, LANES) for e in range(p.col_cycles)]
-    corner[...] = dot(a_full, jnp.concatenate(columns, 1), 0)
-
     gather_d.finish(d_src)
     full = diag.reshape(NB, NB)
     invert(full, inv)
     inv_t[...] = inv[...].T.reshape(inv_t.shape)
+    gather_b.relay()
+    gather_b.finish(b_src)
+    corner[...] += corner_part(cut, p.cycles - 1)
 
     def x_copy(e, k):
         target = (x + k) % p.nx
@@ -274,7 +310,7 @@
             z * p.nx + target,
         )
 
-    inv_tv = inv_t[...].reshape(NB, NB)
+    inv_tv = halves(inv_t[...].reshape(NB, NB))
 
     def put(e, value):
         value = value.reshape(p.owner_z, p.nx, tile, LANES)
@@ -283,8 +319,8 @@
         for k in range(1, p.nx):
             x_copy(e, k).start()
 
-    put(last, dot(inv_tv, corner[:, last * LANES : width]))
-    rest = dot(inv_tv, corner[:, : last * LANES])
+    put(last, dot3(inv_tv, corner[:, last * LANES : width]))
+    rest = dot3(inv_tv, corner[:, : last * LANES])
     for e in range(last):
         put(e, rest[:, e * LANES : (e + 1) * LANES])
 
@@ -316,12 +352,10 @@
     rights = jnp.concatenate(
         [rights[:, : last * LANES], jnp.where(is_panel, unit, rights[:, last * LANES :])], 1
     )
-    spread[...] = dot(inv[...], rights)
-    for e in range(last):
-        x_sum(e)
+    spread[...] = dot3(inv[...], rights)
 
     def trail(begin, end):
-        change = dot(panel[begin:end].reshape((end - begin) * tile, NB), spread[...])
+        change = dot3(panel[begin:end].reshape((end - begin) * tile, NB), spread[...])
         change = change.reshape(end - begin, tile, width)
         for e in range(p.col_cycles):
             part = change[:, :, e * LANES : (e + 1) * LANES]
@@ -332,6 +366,7 @@
 
     middle = (p.cycles - 1) // 2
     trail(0, middle)
+    trail(middle, p.cycles - 1)
 
     def z_sum(e):
         total = ysum[e, owner // p.nx]
@@ -362,7 +397,8 @@
         for copy in start_copies():
             copy.start()
 
-    trail(middle, p.cycles - 1)
+    for e in range(last):
+        x_sum(e)
 
     @pl.when(owner < 0)
     def _():
@@ -384,12 +420,12 @@
         gather_s.start(starts)
         gather_s.relay()
         gather_s.finish(starts)
-        product = dot(full[...], start_full[...].reshape(NB, NB), 0)
+        product = dot3(full[...], start_full[...].reshape(NB, NB), 0)
         row_at, col_at = iota((NB, NB), 0), iota((NB, NB), 1)
         both = (
             jnp.where(row_at >= col_at, product, 0.0) + jnp.where(row_at > col_at, product, 0.0).T
         )
-        changes = dot(dot(inv_t[owner], both), spread[...])
+        changes = dot3(dot3(inv_t[owner], both), spread[...])
         for e in range(last):
             out[0, e] = adjoint[0, e] - z_sum(e) - changes[:, e * LANES : (e + 1) * LANES]
 
@@ -412,6 +448,7 @@
                 copy.wait_send()
 
     gather_a.drain(a_src)
+    gather_b.drain(b_src)
     gather_d.drain(d_src)
     for e in order:
         @pl.when(owner >= 0)
@@ -441,9 +478,12 @@
     result = pl.pallas_call(
         functools.partial(kernel, p),
         out_shape=jax.ShapeDtypeStruct(factor.shape, jnp.float32),
-        in_specs=[pl.BlockSpec(memory_space=pltpu.VMEM)] * 2,
+        in_specs=[pl.BlockSpec(memory_space=pltpu.HBM)] * 2,
         out_specs=pl.BlockSpec(memory_space=pltpu.VMEM),
         scratch_shapes=[
+            pltpu.VMEM(factor.shape, jnp.float32),
+            pltpu.VMEM(factor.shape, jnp.float32),
+            dma((2,)),
             vmem(n, tile, NB),
             vmem(p.owners, tile, cc * LANES),
             vmem(p.owners, tile, NB),
@@ -457,13 +497,13 @@
             vmem(cc, p.nz, tile, LANES),
             vmem(p.owners, tile, LANES),
             vmem(p.owners, tile, NB),
-            *column, *column, *column,
+            *column, *column, *column, *column,
             dma((cc, p.nz)), dma((cc, p.nx)), dma((cc, p.owner_z, p.nx)), dma((cc, p.owners)),
             dma((cc, p.nx)), dma((cc, p.nx)), dma((cc, p.owner_z)), dma((cc, p.nz)),
             dma((p.owners,)), dma((p.owners,)),
         ],
         compiler_params=pltpu.CompilerParams(
-            collective_id=0, has_side_effects=True, vmem_limit_bytes=48 * 1024 * 1024
+            collective_id=0, has_side_effects=True, vmem_limit_bytes=67043328
         ),
     )(factor, adjoint)
     return jnp.transpose(result, (0, 2, 1, 3))

time: 68.8 us -> 68.3 us (level)
  local copies, waits for them, and re-layouts: 4.16 us -> 2.87 us
    unnamed x5 -> x1, local copies, waits for them, and re-layouts: 4.16 us -> 2.87 us
where the time goes in v2:
time: 68.3 us; the launch traced here: 67.7 us
  Pallas kernels  64.8 us (95%)
  local copies, waits for them, and re-layouts  2.87 us (4%)
    pallas_call x1, Pallas kernels, local(): pl.pallas_call(functools.partial(kernel, p), out_shape=jax.ShapeDtypeStru...  64.8 us
    unnamed x1, local copies, waits for them, and re-layouts  2.87 us

profile of v2, /device:TPU:19, one launch (start us, length us, event | category | flops | bytes accessed | tf_op | source)
XLA Modules:
  0.0 67.7 jit_solution(10386487709013421973)
XLA Ops:
  0.0 64.8 %shard_map.28 = f32[9,3,128,128]{3,2,1,0:T(8,128)} custom-call(f32[9,3,128,128]{3,2,1,0:T(8,128)} %bitcast.4, f32[9,3,128,128]{3,2,1,0:T(8,128)} %bitcast.5), custom_call_target="tpu_custom_call" | custom-call | tf_op jit(solution)/shard_map/pallas_call | solution.py:478
  64.8 2.9 %copy.4 = f32[9,128,3,128]{3,1,2,0:T(8,128)} copy(f32[9,128,3,128]{3,1,2,0:T(8,128)} %bitcast.3) | data formatting | bytes 3538944

commit v3 on v2

--- a/solution.py
+++ b/solution.py
@@ -176,6 +176,7 @@
     a_send, a_pair, a_fwd, a_recv, b_send, b_pair, b_fwd, b_recv, d_send, d_pair, d_fwd, d_recv,
     s_send, s_pair, s_fwd, s_recv,
     t_z, t_x, t_fwd, t_recv, x_send, x_recv, z_send, z_recv, r_send, r_recv,
+    low, low_send, low_recv,
 ):
     p = plan
     row, col = lax.axis_index("row"), lax.axis_index("col")
@@ -339,10 +340,32 @@
             ).wait_recv()
             total = total + xrecv[e, source]
         ysum[e] = total
+
+        @pl.when((z == 0) | (z >= first_z))
+        def _():
+            pass_on(e)
+
+    def low_copy(e):
+        return to_row(
+            ysum.at[e], low.at[e], low_send.at[e], low_recv.at[e], (z + 1) % p.nz * p.nx + x
+        )
+
+    def pass_on(e):
+        @pl.when(z < first_z - 1)
+        def _():
+            low_copy(e).start()
+
         for zi in range(p.owner_z):
-            @pl.when(z != first_z + zi)
+            @pl.when((z >= first_z - 1) & (z != first_z + zi))
             def _():
                 z_copy(e, zi).start()
+
+    def fold(e):
+        @pl.when((z > 0) & (z < first_z))
+        def _():
+            low_copy(e).wait_recv()
+            ysum[e] += low[e]
+            pass_on(e)
 
     x_sum(last)
     for e in range(last):
@@ -367,11 +390,14 @@
     middle = (p.cycles - 1) // 2
     trail(0, middle)
     trail(middle, p.cycles - 1)
+    fold(last)
 
     def z_sum(e):
-        total = ysum[e, owner // p.nx]
-        for k in range(1, p.nz):
-            source = (z + k) % p.nz
+        mine_z = owner // p.nx
+        total = ysum[e, mine_z]
+        sources = [first_z - 1] if first_z else []
+        sources += [first_z + (mine_z + k) % p.owner_z for k in range(1, p.owner_z)]
+        for source in sources:
             to_row(
                 zrecv.at[e, source], zrecv.at[e, source], z_send.at[e, 0], z_recv.at[e, source], row
             ).wait_recv()
@@ -389,16 +415,26 @@
         ]
 
     lower = iota((tile, LANES), 0) + owner * tile >= iota((tile, LANES), 1) + mine * LANES
-    gather_s = ColumnGather(p, col, start_full, s_send, s_pair, s_fwd, s_recv)
+    gathers = []
+    for k in range(p.owners):
+        index = (owner + k) % p.owners
+        block = pl.ds(index, 1)
+        gather = ColumnGather(
+            p, col, start_full.at[block], s_send.at[k], s_pair.at[k], s_fwd.at[k], s_recv.at[index]
+        )
+        gathers.append((gather, starts.at[block]))
 
     @pl.when((owner >= 0) & is_panel)
     def _():
         starts[owner] = jnp.where(lower, adjoint[0, last] - z_sum(last), 0.0)
         for copy in start_copies():
             copy.start()
+        gathers[0][0].start(gathers[0][1])
 
     for e in range(last):
         x_sum(e)
+    for e in range(last):
+        fold(e)
 
     @pl.when(owner < 0)
     def _():
@@ -409,17 +445,21 @@
 
     @pl.when(owner >= 0)
     def _():
-        @pl.when(is_panel)
-        def _():
-            for k in range(1, p.owners):
+        for k, (gather, src) in enumerate(gathers):
+            if k:
                 source = (owner + k) % p.owners
-                to_row(
-                    starts.at[source], starts.at[source], r_send.at[k], r_recv.at[source], row
-                ).wait_recv()
-
-        gather_s.start(starts)
-        gather_s.relay()
-        gather_s.finish(starts)
+
+                @pl.when(is_panel)
+                def _():
+                    to_row(
+                        starts.at[source], starts.at[source], r_send.at[k], r_recv.at[source], row
+                    ).wait_recv()
+
+                gather.start(src)
+                gathers[k - 1][0].relay()
+        gathers[-1][0].relay()
+        for gather, src in gathers:
+            gather.finish(src)
         product = dot3(full[...], start_full[...].reshape(NB, NB), 0)
         row_at, col_at = iota((NB, NB), 0), iota((NB, NB), 1)
         both = (
@@ -440,7 +480,8 @@
         def _():
             out[0, last] = adjoint[0, last] - z_sum(last) - part
 
-        gather_s.drain(starts)
+        for gather, src in gathers:
+            gather.drain(src)
 
         @pl.when(is_panel)
         def _():
@@ -459,9 +500,13 @@
         for zi in range(p.owner_z):
             top_forward(e, zi, lambda copy, k: copy.wait_send())
 
-            @pl.when(z != first_z + zi)
+            @pl.when((z >= first_z - 1) & (z != first_z + zi))
             def _():
                 z_copy(e, zi).wait_send()
+
+        @pl.when(z < first_z - 1)
+        def _():
+            low_copy(e).wait_send()
 
         for k in range(1, p.nx):
             x_copy(e, k).wait_send()
@@ -497,10 +542,13 @@
             vmem(cc, p.nz, tile, LANES),
             vmem(p.owners, tile, LANES),
             vmem(p.owners, tile, NB),
-            *column, *column, *column, *column,
+            *column, *column, *column,
+            dma((p.owners, p.ny)), dma((p.owners,)), dma((p.owners, p.ny)),
+            dma((p.owners, p.panels)),
             dma((cc, p.nz)), dma((cc, p.nx)), dma((cc, p.owner_z, p.nx)), dma((cc, p.owners)),
             dma((cc, p.nx)), dma((cc, p.nx)), dma((cc, p.owner_z)), dma((cc, p.nz)),
             dma((p.owners,)), dma((p.owners,)),
+            vmem(cc, p.owner_z, tile, LANES), dma((cc,)), dma((cc,)),
         ],
         compiler_params=pltpu.CompilerParams(
             collective_id=0, has_side_effects=True, vmem_limit_bytes=67043328

time: 68.3 us -> 67.4 us (0.987)
  no operation moved by 1% of the time
where the time goes in v3:
time: 67.4 us; the launch traced here: 67.3 us
  Pallas kernels  64.4 us (96%)
  local copies, waits for them, and re-layouts  2.87 us (4%)
    pallas_call x1, Pallas kernels, local(): pl.pallas_call(functools.partial(kernel, p), out_shape=jax.ShapeDtypeStru...  64.4 us
    unnamed x1, local copies, waits for them, and re-layouts  2.87 us

profile of v3, /device:TPU:19, one launch (start us, length us, event | category | flops | bytes accessed | tf_op | source)
XLA Modules:
  0.0 67.3 jit_solution(4445285937953040311)
XLA Ops:
  0.0 64.4 %shard_map.28 = f32[9,3,128,128]{3,2,1,0:T(8,128)} custom-call(f32[9,3,128,128]{3,2,1,0:T(8,128)} %bitcast.4, f32[9,3,128,128]{3,2,1,0:T(8,128)} %bitcast.5), custom_call_target="tpu_custom_call" | custom-call | tf_op jit(solution)/shard_map/pallas_call | solution.py:523
  64.4 2.9 %copy.4 = f32[9,128,3,128]{3,1,2,0:T(8,128)} copy(f32[9,128,3,128]{3,1,2,0:T(8,128)} %bitcast.3) | data formatting | bytes 3538944
